TPU v7x, 128 devices: a whole 4x4x4 slice. The times are simulated.
128 devices in a mesh: blk: 16 (over z_lo, y, core), seq: 8 (over x, z_hi).
Axes of the slice: x: 4, y: 4, z: 4 (z_hi: 2, z_lo: 2; z = z_hi * 2 + z_lo), core: 2. Of those that a mesh axis runs over, the one named last changes fastest.
Arguments:
- layer_input: bfloat16 [16, 1024, 8192], P('blk', 'seq'), may hold values from -6 to 6
- queries: bfloat16 [16, 1024, 4096], P('blk', 'seq'), may hold values from -48 to 48, as said below
- grad_out: bfloat16 [16, 1024, 4096], P('blk', 'seq'), may hold values from -6 to 6
- segment_ids: int32 [16, 1024], P('blk', 'seq'), may hold values from 0 to 3, never falling along the last dimension, each value on 1 to 512 neighbouring positions
- kv_weight: bfloat16 [8192, 1024], P(('blk', 'seq')), may hold values from -0.0625 to 0.0625
- norm_gain: float32 [8192], replicated, may hold values from 0.5 to 1.5
Outputs:
- attended: bfloat16 [16, 1024, 4096], P('blk', 'seq')
- grad_queries: bfloat16 [16, 1024, 4096], P('blk', 'seq')
- grad_input: bfloat16 [16, 1024, 8192], P('blk', 'seq')
- grad_weight: float32 [8192, 1024], P(('blk', 'seq'))
- grad_gain: float32 [8192], replicated
Inputs may be any that keep to these rules, and one draw needn't show every extreme that they name: Projected queries; some rows may be larger than others.
All inputs are finite; a program needn't handle non-finite values.
Results may differ from a plain program's by a relative error of at most 0.02.
The roundings to bfloat16 on the way count: a program that leaves them out, or rounds other values in their place, can miss the bound.
Values may be sent and summed in bfloat16 or wider, within the bound.
No kernel may reach another device: no remote copies, remote signals or barrier semaphores. Data moves between devices by JAX's collectives and lax.ppermute only.
A program may use at most 128 MiB of HBM per device.

v0:
```python
import jax
import jax.numpy as jnp
from jax import lax
from jax.sharding import PartitionSpec as P

HEAD = 128
epsilon = 1e-05


def cut_along(shard, dim, length):
    lengths = shard.shape
    pieces = shard.reshape(*lengths[:dim], length, lengths[dim] // length, *lengths[dim + 1 :])
    return jnp.moveaxis(pieces, dim, 0)


def sum_at_owner(shard, axis, dim):
    length = lax.axis_size(axis)
    pieces = lax.all_to_all(cut_along(shard, dim, length), axis, 0, 0, tiled=True)
    return jnp.sum(pieces, axis=0)


def shards(layer_input, queries, grad_out, segment_ids, kv_weight, norm_gain):
    f32 = jnp.float32
    tok_rows = layer_input.shape[1]
    model_width = layer_input.shape[2]
    seq_devices = lax.axis_size("seq")
    blk_devices = lax.axis_size("blk")
    length = tok_rows * seq_devices
    seq_index = lax.axis_index("seq")
    kv_total = kv_weight.shape[1]
    kv_width = kv_total // 2
    kv_heads = kv_width // HEAD
    query_count = queries.shape[2] // HEAD
    group_size = query_count // kv_heads
    score_scale = HEAD ** (-0.5)
    piece_cols = kv_weight.shape[0]
    source = layer_input[0].astype(f32)
    inv_rms = lax.rsqrt(jnp.mean(source * source, axis=1, keepdims=True) + epsilon)
    scaled = source * inv_rms
    normed = (scaled * norm_gain).astype(jnp.bfloat16)
    split_cols = normed.reshape(tok_rows, blk_devices, seq_devices, piece_cols)
    columns = lax.all_to_all(split_cols, "seq", split_axis=2, concat_axis=0, tiled=True).reshape(
        length, blk_devices * piece_cols
    )
    weight_slab = lax.all_gather(kv_weight, "blk", axis=0, tiled=True)
    query_heads = queries[0].reshape(tok_rows, kv_heads, group_size, HEAD)
    query_pos = seq_index * tok_rows + jnp.arange(tok_rows, dtype=jnp.int32)
    query_doc = segment_ids[0]
    grad_heads = grad_out[0].reshape(tok_rows, kv_heads, group_size, HEAD).transpose(1, 2, 0, 3)

    def scores_of(kv_piece, doc_piece):
        rows_here = kv_piece.shape[0]
        key_heads = kv_piece[:, :kv_width].reshape(rows_here, kv_heads, HEAD)
        raw_scores = (
            jnp.einsum("qgjd,kgd->gjqk", query_heads, key_heads, preferred_element_type=f32)
            * score_scale
        )
        key_pos = jnp.arange(rows_here, dtype=jnp.int32)
        allowed = (key_pos[None, :] <= query_pos[:, None]) & (
            doc_piece[None, :] == query_doc[:, None]
        )
        return (jnp.where(allowed, raw_scores, -1e30), allowed, key_heads)

    stat_shape = (kv_heads, group_size, tok_rows, 1)
    kv_own = sum_at_owner(
        jnp.dot(columns, weight_slab, preferred_element_type=f32), "seq", 0
    ).astype(jnp.bfloat16)
    row_max = jnp.full(stat_shape, -1e30, f32)
    kv_piece = lax.all_gather(kv_own, "seq", axis=0, tiled=True)
    doc_piece = lax.all_gather(query_doc, "seq", axis=0, tiled=True)
    rows_here = kv_piece.shape[0]
    masked, allowed, key_heads = scores_of(kv_piece, doc_piece)
    new_max = jnp.maximum(row_max, jnp.max(masked, axis=-1, keepdims=True))
    expo_terms = jnp.where(allowed, jnp.exp(masked - new_max), 0.0)
    value_heads = kv_piece[:, kv_width:].reshape(rows_here, kv_heads, HEAD)
    weights = expo_terms.astype(jnp.bfloat16)
    weighted = jnp.einsum("gjqk,kgd->gjqd", weights, value_heads, preferred_element_type=f32)
    row_sum = jnp.sum(expo_terms, axis=-1, keepdims=True)
    row_max, row_sum, weighted = (new_max, row_sum, weighted)
    summed = weighted / row_sum
    attended = (
        summed.transpose(2, 0, 1, 3).reshape(tok_rows, query_count * HEAD).astype(jnp.bfloat16)
    )
    log_total = row_max + jnp.log(row_sum)
    attended_heads = attended.reshape(tok_rows, kv_heads, group_size, HEAD).transpose(1, 2, 0, 3)
    row_delta = jnp.sum(grad_heads.astype(f32) * attended_heads.astype(f32), axis=-1, keepdims=True)
    kv_piece = lax.all_gather(kv_own, "seq", axis=0, tiled=True)
    doc_piece = lax.all_gather(query_doc, "seq", axis=0, tiled=True)
    rows_here = kv_piece.shape[0]
    masked, allowed, key_heads = scores_of(kv_piece, doc_piece)
    softmax_probs = jnp.where(allowed, jnp.exp(masked - log_total), 0.0)
    value_heads = kv_piece[:, kv_width:].reshape(rows_here, kv_heads, HEAD)
    grad_probs = jnp.einsum("gjqd,kgd->gjqk", grad_heads, value_heads, preferred_element_type=f32)
    grad_scores = (softmax_probs * (grad_probs - row_delta)).astype(jnp.bfloat16)
    probs_half = softmax_probs.astype(jnp.bfloat16)
    grad_values = jnp.einsum("gjqk,gjqd->kgd", probs_half, grad_heads, preferred_element_type=f32)
    grad_keys = (
        jnp.einsum("gjqk,qgjd->kgd", grad_scores, query_heads, preferred_element_type=f32)
        * score_scale
    )
    grad_query = (
        jnp.einsum("gjqk,kgd->qgjd", grad_scores, key_heads, preferred_element_type=f32)
        * score_scale
    )
    new_rows = jnp.concatenate(
        [grad_keys.reshape(rows_here, kv_width), grad_values.reshape(rows_here, kv_width)], axis=1
    )
    grad_rows = new_rows
    grad_query, grad_rows = (grad_query, grad_rows)
    grad_own = sum_at_owner(grad_rows, "seq", 0).astype(jnp.bfloat16)
    grad_kv = lax.all_gather(grad_own, "seq", axis=0, tiled=True)
    grad_queries = grad_query.reshape(tok_rows, query_count * HEAD).astype(jnp.bfloat16)
    slab_back = lax.all_gather(kv_weight, "blk", axis=0, tiled=True)
    grad_weight = lax.psum_scatter(
        lax.dot_general(columns, grad_kv, (((0,), (0,)), ((), ())), preferred_element_type=f32),
        "blk",
        scatter_dimension=0,
        tiled=True,
    )
    grad_cols = lax.dot_general(
        grad_kv, slab_back, (((1,), (1,)), ((), ())), preferred_element_type=f32
    ).astype(jnp.bfloat16)
    grad_cols = grad_cols.reshape(length, blk_devices, 1, piece_cols)
    grad_normed = lax.all_to_all(grad_cols, "seq", split_axis=0, concat_axis=2, tiled=True).reshape(
        tok_rows, model_width
    )
    grad_norm = grad_normed.astype(f32)
    grad_gain = lax.psum(jnp.sum(grad_norm * scaled, axis=0), ("blk", "seq"))
    grad_hat = grad_norm * norm_gain
    grad_input = inv_rms * (grad_hat - scaled * jnp.mean(grad_hat * scaled, axis=1, keepdims=True))
    return (
        attended[None],
        grad_queries[None],
        grad_input.astype(jnp.bfloat16)[None],
        grad_weight,
        grad_gain,
    )


def solution(mesh):
    in_specs = (
        P("blk", "seq", None),
        P("blk", "seq", None),
        P("blk", "seq", None),
        P("blk", "seq"),
        P(("blk", "seq"), None),
        P(),
    )
    out_specs = (
        P("blk", "seq", None),
        P("blk", "seq", None),
        P("blk", "seq", None),
        P(("blk", "seq"), None),
        P(),
    )
    return jax.shard_map(shards, mesh=mesh, in_specs=in_specs, out_specs=out_specs, check_vma=False)
```

profile of v0, /device:TPU:1, one launch (start us, length us, event | category | flops | bytes accessed | tf_op | source)
XLA Modules:
  0.0 534.6 jit_solution(473694179402004484)
XLA Ops:
  7.2 0.0 all-gather.5.cloned.1.call-start
  7.2 0.7 all-gather.5.cloned.1.call-update
  7.9 0.0 all-gather.7.cloned.1.call-start
  8.0 3.2 copy.148
  11.2 2.2 convert_element_type.140
  13.4 0.1 mul.121
  13.5 1.1 multiply_reduce_fusion.2
  14.6 2.9 multiply_convert_fusion
  17.5 0.2 copy.149
  17.7 38.3 %all_to_all.34 = bf16[128,16,8,64]{0,3,1,2:T(8,128)(2,1)} all-to-all(bf16[128,16,8,64]{0,3,1,2:T(8,128)(2,1)S(1)} %copy.149), channel_id=1, replica_groups=mesh['blk'=16,'seq'=8] {'seq'}, dimensions={2} | all-to-all | bytes 4194304 | tf_op jit(solution)/shard_map/all_to_all | solution.py:42
  56.0 8.3 %all-gather.5.cloned.1.call-done = bf16[1024,1024]{1,0:T(8,128)(2,1)} async-done(((bf16[64,1024]{1,0:T(8,128)(2,1)}), bf16[1024,1024]{1,0:T(8,128)(2,1)}) %all-gather.5.cloned.1.call-update) | async-done | bytes 2097168 | tf_op jit(solution)/shard_map/all_gather | solution.py:45
  64.3 4.6 fusion.22
  68.9 55.1 %all_to_all.35 = f32[8,128,1024]{2,1,0:T(8,128)} all-to-all(f32[8,128,1024]{2,1,0:T(8,128)S(1)} %fusion.22), channel_id=1, replica_groups=mesh['blk'=16,'seq'=8] {'seq'}, dimensions={0} | all-to-all | bytes 8388608 | tf_op jit(solution)/shard_map/all_to_all | solution.py:18
  124.1 3.4 reduce_sum.66
  127.5 0.0 all-gather.9.cloned.1.call-start
  127.6 1.2 copy.192
  128.8 2.3 copy.156
  131.0 17.1 %all-gather = s32[1,1024]{1,0:T(1,128)S(1)} all-gather(s32[1,128]{1,0:T(1,128)S(1)} %copy-done.8), channel_id=2, replica_groups=mesh['blk'=16,'seq'=8] {'seq'}, dimensions={1}, use_global_device_ids=true | all-gather | bytes 4608 | tf_op jit(solution)/shard_map/all_gather | solution.py:70
  148.2 0.2 fusion.29
  148.4 30.2 %all-gather.7.cloned.1.call-done = bf16[1024,1024]{1,0:T(8,128)(2,1)} async-done(((bf16[128,1024]{1,0:T(8,128)(2,1)}), bf16[1024,1024]{1,0:T(8,128)(2,1)}) %all-gather.7.cloned.1.call-update) | async-done | bytes 2097168 | tf_op jit(solution)/shard_map/all_gather | solution.py:69
  178.5 3.0 fusion.32
  181.5 1.5 copy.151
  183.0 9.1 %fusion.33 = (f32[4,8,128]{2,1,0:T(8,128)S(1)}, f32[4,8,128,1024]{2,3,1,0:T(8,128)}) fusion(bf16[1024,4,128,1]{0,2,3,1:T(8,128)(2,1)S(1)} %bitcast.122, bf16[128,4,8,128]{3,2,1,0:T(8,128)(2,1)} %bitcast.124, pred[128,1024]{0,1:T(8,128)(4,1)S(1)} %fusion.29), kind=kOutput, calls=%fused_computation.52 | convolution fusion | flops 1086320640 | bytes 19021824 | tf_op jit(solution)/shard_map/qgjd,kgd->gjqk/dot_general | solution.py:55
  192.1 2.3 copy.154
  194.4 8.7 %fusion.1 = f32[4,8,128]{2,1,0:T(8,128)S(1)} fusion(f32[4,8,128,1024]{2,3,1,0:T(8,128)} %get-tuple-element.45, f32[4,8,128]{2,1,0:T(8,128)S(1)} %broadcast_maximum_fusion, pred[128,1024]{0,1:T(8,128)(4,1)S(1)} %fusion.29), kind=kLoop, calls=%fused_computation.5 | loop fusion | flops 12578816 | bytes 16941056 | tf_op jit(solution)/shard_map/reduce_sum | solution.py:78
  203.1 9.9 %fusion.21 = (bf16[128,4,8,128]{0,3,2,1:T(8,128)(2,1)}, f32[4,8,128,128]{2,3,1,0:T(8,128)S(1)}) fusion(f32[128,4,8]{0,2,1:T(8,128)S(1)} %bitcast.140, bf16[1024,4,128,1]{0,2,3,1:T(8,128)(2,1)S(1)} %bitcast.138, f32[4,8,128,1024]{2,3,1,0:T(8,128)} %get-tuple-element.45, f32[4,8,128]{2,1,0:T(8,128)S(1)} %broadcast_maximum_fusion, ...), kind=kOutput, calls=%fused_computation.32 | convolution fusion | flops 1087373312 | bytes 21135360 | tf_op jit(solution)/shard_map/gjqk,kgd->gjqd/dot_general | solution.py:77
  212.9 0.5 multiply_reduce_fusion.3
  213.4 9.5 %fusion.24 = f32[1024,4,128]{2,0,1:T(8,128)} fusion(bf16[4,8,128,128]{2,3,1,0:T(8,128)(2,1)S(1)} %bitcast.131, f32[4,8,128,1024]{2,3,1,0:T(8,128)} %get-tuple-element.45, f32[4,8,128]{2,1,0:T(8,128)S(1)} %log_add_fusion, pred[128,1024]{0,1:T(8,128)(4,1)S(1)} %fusion.29), kind=kOutput, calls=%fused_computation.39 | convolution fusion | flops 1086324736 | bytes 20070400 | tf_op jit(solution)/shard_map/gjqk,gjqd->kgd/dot_general | solution.py:96
  222.9 10.9 %fusion = bf16[4,8,128,1024]{2,3,1,0:T(8,128)(2,1)} fusion(f32[4,8,128,1024]{2,3,1,0:T(8,128)} %get-tuple-element.45, bf16[1024,4,128,1]{0,2,3,1:T(8,128)(2,1)S(1)} %bitcast.139, bf16[4,8,128,128]{2,3,1,0:T(8,128)(2,1)S(1)} %bitcast.132, f32[4,8,128]{2,1,0:T(8,128)S(1)} %multiply_reduce_fusion.3, f32[4,8,128]{2,1,0:T(8,128)S(1)} %log_add_fusion, ...), kind=kOutput, calls=%fused_computation.1 | convolution fusion | flops 1094713344 | bytes 27426816 | tf_op jit(solution)/shard_map/gjqd,kgd->gjqk/dot_general | solution.py:93
  233.8 2.9 copy.163
  236.7 3.5 copy.194
  240.2 7.1 %fusion.20 = f32[1024,4,128]{2,0,1:T(8,128)} fusion(bf16[4,8,128,1024]{2,3,1,0:T(8,128)(2,1)} %fusion, bf16[128,4,8,128]{3,2,1,0:T(8,128)(2,1)S(1)} %bitcast.125), kind=kOutput, calls=%fused_computation.30 | convolution fusion | flops 1074266112 | bytes 11534336 | tf_op jit(solution)/shard_map/gjqk,qgjd->kgd/dot_general | solution.py:98
  247.3 2.9 copy.161
  250.2 2.2 copy.193
  252.4 0.3 pad_maximum_fusion
  252.7 0.8 copy.164
  253.5 50.9 %all_to_all.36 = f32[8,128,1024]{1,2,0:T(8,128)} all-to-all(f32[8,128,1024]{1,2,0:T(8,128)S(1)} %copy.164), channel_id=1, replica_groups=mesh['blk'=16,'seq'=8] {'seq'}, dimensions={0} | all-to-all | bytes 8388608 | tf_op jit(solution)/shard_map/all_to_all | solution.py:18
  304.4 3.2 reduce_sum.69
  307.6 0.2 reduce-scatter.2.cloned.1.call-start
  307.8 4.7 copy.171
  312.5 51.4 %all-gather.9.cloned.1.call-done = bf16[1024,1024]{0,1:T(8,128)(2,1)} async-done(((bf16[128,1024]{0,1:T(8,128)(2,1)}), bf16[1024,1024]{0,1:T(8,128)(2,1)}) %all-gather.9.cloned.1.call-update) | async-done | bytes 2097168 | tf_op jit(solution)/shard_map/all_gather | solution.py:111
  363.9 6.5 %fusion.17 = f32[1024,1024]{1,0:T(8,128)} fusion(bf16[1024,1024]{0,1:T(8,128)(2,1)} %all-gather.9.cloned.1.call-done, bf16[128,8,8,128]{3,2,1,0:T(8,128)(2,1)} %bitcast.135), kind=kOutput, calls=%fused_computation.26 | convolution fusion | flops 2147483648 | bytes 8388608 | tf_op jit(solution)/shard_map/dot_general | solution.py:115
  370.4 5.9 %convolution_convert_fusion = bf16[1024,1024]{0,1:T(8,128)(2,1)} fusion(bf16[1024,1024]{1,0:T(8,128)(2,1)} %all-gather.5.cloned.1.call-done, bf16[1024,1024]{0,1:T(8,128)(2,1)} %all-gather.9.cloned.1.call-done), kind=kOutput, calls=%fused_computation.38 | convolution fusion | flops 2148532224 | bytes 6291456 | tf_op jit(solution)/shard_map/dot_general | solution.py:120
  376.3 6.2 %copy.166 = bf16[1024,16,1,64]{3,1,2,0:T(8,128)(2,1)} copy(bf16[1024,16,1,64]{0,3,1,2:T(8,128)(2,1)} %bitcast.134) | data formatting | bytes 4194304 | tf_op jit(solution)/shard_map/reshape | solution.py:123
  382.5 7.6 %reshape.223 = bf16[8,2,65536]{2,1,0:T(2,128)(2,1)} reshape(bf16[1024,1,16,64]{3,2,1,0:T(8,128)(2,1)} %bitcast.119) | data formatting | bytes 4194304
  390.1 4.6 all-to-all-start.3
  394.6 1.0 copy.169
  395.7 2.3 copy.173
  397.9 5.6 %multiply_convert_fusion.1 = bf16[4,128,8,128]{3,1,2,0:T(8,128)(2,1)} fusion(bf16[1024,4,128,1]{0,2,3,1:T(8,128)(2,1)S(1)} %bitcast.123, bf16[4,8,128,1024]{2,3,1,0:T(8,128)(2,1)} %fusion), kind=kOutput, calls=%fused_computation.35 | convolution fusion | flops 1074790400 | bytes 10485760 | tf_op jit(solution)/shard_map/gjqk,kgd->qgjd/dot_general | solution.py:102
  403.6 2.3 copy.174
  405.9 22.6 %all-to-all-done.3 = bf16[8,2,65536]{2,1,0:T(2,128)(2,1)} async-done(((bf16[8,2,65536]{2,1,0:T(2,128)(2,1)}), bf16[8,2,65536]{2,1,0:T(2,128)(2,1)}, u32[]{:S(2)}, u32[]{:S(2)}) %all-to-all-start.3) | async-done | bytes 2097184 | tf_op jit(solution)/shard_map/all_to_all | solution.py:124
  428.4 7.4 %reshape.224 = bf16[1024,1,16,64]{3,2,1,0:T(8,128)(2,1)} reshape(bf16[8,2,65536]{2,1,0:T(2,128)(2,1)} %all-to-all-done.3) | data formatting | bytes 4194304
  435.8 5.5 %copy.167 = bf16[1024,16,1,64]{0,3,2,1:T(8,128)(2,1)} copy(bf16[1024,16,1,64]{3,1,2,0:T(8,128)(2,1)} %bitcast.120) | data formatting | bytes 4194304 | tf_op jit(solution)/shard_map/all_to_all | solution.py:124
  441.3 2.1 convert_element_type.146
  443.4 1.0 copy.195
  444.4 0.7 copy.168
  445.2 1.4 copy-done
  446.6 0.1 copy-done.4
  446.7 4.8 multiply_reduce_fusion
  451.5 4.4 fusion.16
  455.9 4.1 copy.175
  460.0 0.2 copy.172
  460.2 0.1 reduce_sum.72
  460.2 67.6 %psum.7 = f32[8192]{0:T(1024)} all-reduce(f32[8192]{0:T(1024)S(1)} %reduce_sum.72), channel_id=1, replica_groups=mesh['blk'=16,'seq'=8] {'blk','seq'}, use_global_device_ids=true, to_apply=%region_9.10 | all-reduce | flops 8192 | bytes 65536 | tf_op jit(solution)/shard_map/psum | solution.py:128
  (25 shorter events, 0.1 us)
Async XLA Ops:
  7.2 57.1 %all-gather.5.cloned.1.call-start = ((), (), s32[]{:S(2)}) async-start(), calls=%async_computation.5 | async-start | bytes 2228224 | tf_op jit(solution)/shard_map/all_gather | solution.py:45
  7.9 5.5 %copy-start.7 = (f32[8192]{0:T(1024)S(1)}, f32[8192]{0:T(1024)}, u32[]{:S(2)}) copy-start(f32[8192]{0:T(1024)} %param.11) | copy-start | bytes 98308
  7.9 170.6 %all-gather.7.cloned.1.call-start = ((), (), s32[]{:S(2)}) async-start(), calls=%async_computation.6 | async-start | bytes 2359296 | tf_op jit(solution)/shard_map/all_gather | solution.py:69
  124.0 3.5 copy-start.5
  124.0 7.0 %copy-start.8 = (s32[1,128]{1,0:T(1,128)S(1)}, s32[1,128]{1,0:T(1,128)}, u32[]{:S(2)}) copy-start(s32[1,128]{1,0:T(1,128)} %param.9) | copy-start | bytes 1540
  127.5 236.4 %all-gather.9.cloned.1.call-start = ((), (), s32[]{:S(2)}) async-start(), calls=%async_computation.7 | async-start | bytes 2359296 | tf_op jit(solution)/shard_map/all_gather | solution.py:111
  194.4 8.7 %copy-start.6 = (bf16[1024,512]{0,1:T(8,128)(2,1)S(1)}, bf16[1024,512]{0,1:T(8,128)(2,1)}, u32[]{:S(2)}) copy-start(bf16[1024,512]{0,1:T(8,128)(2,1)} %copy.154) | copy-start | bytes 3145732
  203.1 9.9 %copy-start.3 = (bf16[1,128,4096]{1,2,0:T(8,128)(2,1)S(1)}, bf16[1,128,4096]{1,2,0:T(8,128)(2,1)}, u32[]{:S(2)}) copy-start(bf16[1,128,4096]{1,2,0:T(8,128)(2,1)} %copy.156) | copy-start | bytes 3145732
  236.7 3.5 copy-start.1
  250.2 2.2 copy-start.2
  307.6 220.3 %reduce-scatter.2.cloned.1.call-start = ((), (), s32[]{:S(2)}) async-start(), calls=%async_computation.8 | async-start | bytes 4456448 | tf_op jit(solution)/shard_map/reduce_scatter | solution.py:114
  390.1 38.4 %all-to-all-start.3 = ((bf16[8,2,65536]{2,1,0:T(2,128)(2,1)}), bf16[8,2,65536]{2,1,0:T(2,128)(2,1)}, u32[]{:S(2)}, u32[]{:S(2)}) async-start(bf16[8,2,65536]{2,1,0:T(2,128)(2,1)} %reshape.223), calls=%async_computation.3 | async-start | bytes 4194304 | tf_op jit(solution)/shard_map/all_to_all | solution.py:124
  444.4 2.2 copy-start
  444.4 2.3 copy-start.4
Sparse Core Ops, SparseCore 0:
  9.7 54.5 all-gather.4
  127.6 50.8 all-gather.6
  307.7 56.0 all-gather.8
  370.5 72.2 reduce-scatter.1
where the time goes:
time: 540 us; the launch traced here: 535 us
  blocking collectives  229 us (42%)
  waiting for transfers between devices  113 us (21%)
  local copies, waits for them, and re-layouts  70.6 us (13%)
  matrix products  69.1 us (13%)
  other arithmetic  33.7 us (6%)
  between operations  14.2 us (3%)
    all_to_all x2, blocking collectives, sum_at_owner(): lax.all_to_all(cut_along(shard, dim, length), axis, 0, 0, tiled=True)  106 us
    psum x1, blocking collectives, shards(): grad_gain = lax.psum(jnp.sum(grad_norm * scaled, axis=0), ('blk', 'seq'))  67.6 us
    all_gather x1, waiting for transfers between devices, shards(): grad_kv = lax.all_gather(grad_own, 'seq', axis=0, tiled=True)  51.4 us
    unnamed x29, local copies, waits for them, and re-layouts  38.6 us
    all_to_all x1, blocking collectives, shards(): lax.all_to_all(split_cols, 'seq', split_axis=2, concat_axis=0, tiled=True)  38.3 us
    all_gather x1, waiting for transfers between devices, shards(): kv_piece = lax.all_gather(kv_own, 'seq', axis=0, tiled=True)  30.2 us
    all_to_all x1, waiting for transfers between devices, shards(): lax.all_to_all(grad_cols, 'seq', split_axis=0, concat_axis=2, tiled=True)  22.6 us
    all_gather x1, blocking collectives, shards(): doc_piece = lax.all_gather(query_doc, 'seq', axis=0, tiled=True)  17.1 us
  transfers between devices with their start and end apart: 5, of which 4 were waited for; matrix products, arithmetic and copies ran while one was open for 15% of the time, Pallas kernels for 0%

commit v1 on v0

--- a/solution.py
+++ b/solution.py
@@ -125,7 +125,7 @@
         tok_rows, model_width
     )
     grad_norm = grad_normed.astype(f32)
-    grad_gain = lax.psum(jnp.sum(grad_norm * scaled, axis=0), ("blk", "seq"))
+    grad_gain = lax.psum(lax.psum(jnp.sum(grad_norm * scaled, axis=0), "blk"), "seq")
     grad_hat = grad_norm * norm_gain
     grad_input = inv_rms * (grad_hat - scaled * jnp.mean(grad_hat * scaled, axis=1, keepdims=True))
     return (

time: 540 us -> 570 us (1.056)
  the two profiles are of different devices: /device:TPU:1 before, /device:TPU:0 now
where the time goes in v1:
time: 570 us; the launch traced here: 564 us
  blocking collectives  264 us (46%)
  waiting for transfers between devices  108 us (19%)
  local copies, waits for them, and re-layouts  70.5 us (12%)
  matrix products  69.1 us (12%)
  other arithmetic  33.7 us (6%)
  between operations  14.2 us (2%)
    all_to_all x2, blocking collectives, sum_at_owner(): lax.all_to_all(cut_along(shard, dim, length), axis, 0, 0, tiled=True)  109 us
    psum x1, blocking collectives, shards(): lax.psum(jnp.sum(grad_norm * scaled, axis=0), 'blk')  53.5 us
    all_gather x1, waiting for transfers between devices, shards(): grad_kv = lax.all_gather(grad_own, 'seq', axis=0, tiled=True)  49.8 us
    psum x1, blocking collectives, shards(): lax.psum(lax.psum(jnp.sum(grad_norm * scaled, axis=0), 'blk'), 'seq')  42.2 us
    all_to_all x1, blocking collectives, shards(): lax.all_to_all(split_cols, 'seq', split_axis=2, concat_axis=0, tiled=True)  38.7 us
    unnamed x29, local copies, waits for them, and re-layouts  38.5 us
    all_gather x1, waiting for transfers between devices, shards(): kv_piece = lax.all_gather(kv_own, 'seq', axis=0, tiled=True)  27.2 us
    all_to_all x1, waiting for transfers between devices, shards(): lax.all_to_all(grad_cols, 'seq', split_axis=0, concat_axis=2, tiled=True)  23.2 us
  transfers between devices with their start and end apart: 5, of which 4 were waited for; matrix products, arithmetic and copies ran while one was open for 14% of the time, Pallas kernels for 0%

profile of v1, /device:TPU:0, one launch (start us, length us, event | category | flops | bytes accessed | tf_op | source)
XLA Modules:
  0.0 564.2 jit_solution(11661650822338504014)
XLA Ops:
  7.2 0.7 all-gather.5.cloned.1.call-update
  7.9 0.0 all-gather.7.cloned.1.call-start
  8.0 3.2 copy.148
  11.2 2.2 convert_element_type.140
  13.4 0.1 mul.121
  13.5 1.1 multiply_reduce_fusion.2
  14.6 2.8 multiply_convert_fusion
  17.5 0.2 copy.149
  17.7 38.7 %all_to_all.34 = bf16[128,16,8,64]{0,3,1,2:T(8,128)(2,1)} all-to-all(bf16[128,16,8,64]{0,3,1,2:T(8,128)(2,1)S(1)} %copy.149), channel_id=1, replica_groups=mesh['blk'=16,'seq'=8] {'seq'}, dimensions={2} | all-to-all | bytes 4194304 | tf_op jit(solution)/shard_map/all_to_all | solution.py:42
  56.4 6.8 %all-gather.5.cloned.1.call-done = bf16[1024,1024]{1,0:T(8,128)(2,1)} async-done(((bf16[64,1024]{1,0:T(8,128)(2,1)}), bf16[1024,1024]{1,0:T(8,128)(2,1)}) %all-gather.5.cloned.1.call-update) | async-done | bytes 2097168 | tf_op jit(solution)/shard_map/all_gather | solution.py:45
  63.2 4.6 fusion.22
  67.8 57.0 %all_to_all.35 = f32[8,128,1024]{2,1,0:T(8,128)} all-to-all(f32[8,128,1024]{2,1,0:T(8,128)S(1)} %fusion.22), channel_id=1, replica_groups=mesh['blk'=16,'seq'=8] {'seq'}, dimensions={0} | all-to-all | bytes 8388608 | tf_op jit(solution)/shard_map/all_to_all | solution.py:18
  124.8 3.4 reduce_sum.66
  128.2 0.0 all-gather.9.cloned.1.call-start
  128.3 1.2 copy.192
  129.5 2.3 copy.156
  131.8 20.2 %all-gather = s32[1,1024]{1,0:T(1,128)S(1)} all-gather(s32[1,128]{1,0:T(1,128)S(1)} %copy-done.8), channel_id=2, replica_groups=mesh['blk'=16,'seq'=8] {'seq'}, dimensions={1}, use_global_device_ids=true | all-gather | bytes 4608 | tf_op jit(solution)/shard_map/all_gather | solution.py:70
  152.0 0.2 fusion.29
  152.2 27.2 %all-gather.7.cloned.1.call-done = bf16[1024,1024]{1,0:T(8,128)(2,1)} async-done(((bf16[128,1024]{1,0:T(8,128)(2,1)}), bf16[1024,1024]{1,0:T(8,128)(2,1)}) %all-gather.7.cloned.1.call-update) | async-done | bytes 2097168 | tf_op jit(solution)/shard_map/all_gather | solution.py:69
  179.4 3.0 fusion.32
  182.4 1.5 copy.151
  183.9 9.1 %fusion.33 = (f32[4,8,128]{2,1,0:T(8,128)S(1)}, f32[4,8,128,1024]{2,3,1,0:T(8,128)}) fusion(bf16[1024,4,128,1]{0,2,3,1:T(8,128)(2,1)S(1)} %bitcast.122, bf16[128,4,8,128]{3,2,1,0:T(8,128)(2,1)} %bitcast.124, pred[128,1024]{0,1:T(8,128)(4,1)S(1)} %fusion.29), kind=kOutput, calls=%fused_computation.52 | convolution fusion | flops 1086320640 | bytes 19021824 | tf_op jit(solution)/shard_map/qgjd,kgd->gjqk/dot_general | solution.py:55
  193.0 2.3 copy.154
  195.2 8.7 %fusion.1 = f32[4,8,128]{2,1,0:T(8,128)S(1)} fusion(f32[4,8,128,1024]{2,3,1,0:T(8,128)} %get-tuple-element.45, f32[4,8,128]{2,1,0:T(8,128)S(1)} %broadcast_maximum_fusion, pred[128,1024]{0,1:T(8,128)(4,1)S(1)} %fusion.29), kind=kLoop, calls=%fused_computation.5 | loop fusion | flops 12578816 | bytes 16941056 | tf_op jit(solution)/shard_map/reduce_sum | solution.py:78
  203.9 9.9 %fusion.21 = (bf16[128,4,8,128]{0,3,2,1:T(8,128)(2,1)}, f32[4,8,128,128]{2,3,1,0:T(8,128)S(1)}) fusion(f32[128,4,8]{0,2,1:T(8,128)S(1)} %bitcast.140, bf16[1024,4,128,1]{0,2,3,1:T(8,128)(2,1)S(1)} %bitcast.138, f32[4,8,128,1024]{2,3,1,0:T(8,128)} %get-tuple-element.45, f32[4,8,128]{2,1,0:T(8,128)S(1)} %broadcast_maximum_fusion, ...), kind=kOutput, calls=%fused_computation.32 | convolution fusion | flops 1087373312 | bytes 21135360 | tf_op jit(solution)/shard_map/gjqk,kgd->gjqd/dot_general | solution.py:77
  213.8 0.5 multiply_reduce_fusion.3
  214.3 9.5 %fusion.24 = f32[1024,4,128]{2,0,1:T(8,128)} fusion(bf16[4,8,128,128]{2,3,1,0:T(8,128)(2,1)S(1)} %bitcast.131, f32[4,8,128,1024]{2,3,1,0:T(8,128)} %get-tuple-element.45, f32[4,8,128]{2,1,0:T(8,128)S(1)} %log_add_fusion, pred[128,1024]{0,1:T(8,128)(4,1)S(1)} %fusion.29), kind=kOutput, calls=%fused_computation.39 | convolution fusion | flops 1086324736 | bytes 20070400 | tf_op jit(solution)/shard_map/gjqk,gjqd->kgd/dot_general | solution.py:96
  223.8 10.9 %fusion = bf16[4,8,128,1024]{2,3,1,0:T(8,128)(2,1)} fusion(f32[4,8,128,1024]{2,3,1,0:T(8,128)} %get-tuple-element.45, bf16[1024,4,128,1]{0,2,3,1:T(8,128)(2,1)S(1)} %bitcast.139, bf16[4,8,128,128]{2,3,1,0:T(8,128)(2,1)S(1)} %bitcast.132, f32[4,8,128]{2,1,0:T(8,128)S(1)} %multiply_reduce_fusion.3, f32[4,8,128]{2,1,0:T(8,128)S(1)} %log_add_fusion, ...), kind=kOutput, calls=%fused_computation.1 | convolution fusion | flops 1094713344 | bytes 27426816 | tf_op jit(solution)/shard_map/gjqd,kgd->gjqk/dot_general | solution.py:93
  234.6 2.9 copy.163
  237.6 3.5 copy.194
  241.0 7.1 %fusion.20 = f32[1024,4,128]{2,0,1:T(8,128)} fusion(bf16[4,8,128,1024]{2,3,1,0:T(8,128)(2,1)} %fusion, bf16[128,4,8,128]{3,2,1,0:T(8,128)(2,1)S(1)} %bitcast.125), kind=kOutput, calls=%fused_computation.30 | convolution fusion | flops 1074266112 | bytes 11534336 | tf_op jit(solution)/shard_map/gjqk,qgjd->kgd/dot_general | solution.py:98
  248.1 2.9 copy.161
  251.0 2.2 copy.193
  253.2 0.3 pad_maximum_fusion
  253.5 0.8 copy.164
  254.3 52.5 %all_to_all.36 = f32[8,128,1024]{1,2,0:T(8,128)} all-to-all(f32[8,128,1024]{1,2,0:T(8,128)S(1)} %copy.164), channel_id=1, replica_groups=mesh['blk'=16,'seq'=8] {'seq'}, dimensions={0} | all-to-all | bytes 8388608 | tf_op jit(solution)/shard_map/all_to_all | solution.py:18
  306.9 3.2 reduce_sum.69
  310.1 0.2 reduce-scatter.2.cloned.1.call-start
  310.3 4.7 copy.171
  315.0 49.8 %all-gather.9.cloned.1.call-done = bf16[1024,1024]{0,1:T(8,128)(2,1)} async-done(((bf16[128,1024]{0,1:T(8,128)(2,1)}), bf16[1024,1024]{0,1:T(8,128)(2,1)}) %all-gather.9.cloned.1.call-update) | async-done | bytes 2097168 | tf_op jit(solution)/shard_map/all_gather | solution.py:111
  364.7 6.5 %fusion.17 = f32[1024,1024]{1,0:T(8,128)} fusion(bf16[1024,1024]{0,1:T(8,128)(2,1)} %all-gather.9.cloned.1.call-done, bf16[128,8,8,128]{3,2,1,0:T(8,128)(2,1)} %bitcast.135), kind=kOutput, calls=%fused_computation.26 | convolution fusion | flops 2147483648 | bytes 8388608 | tf_op jit(solution)/shard_map/dot_general | solution.py:115
  371.3 5.9 %convolution_convert_fusion = bf16[1024,1024]{0,1:T(8,128)(2,1)} fusion(bf16[1024,1024]{1,0:T(8,128)(2,1)} %all-gather.5.cloned.1.call-done, bf16[1024,1024]{0,1:T(8,128)(2,1)} %all-gather.9.cloned.1.call-done), kind=kOutput, calls=%fused_computation.38 | convolution fusion | flops 2148532224 | bytes 6291456 | tf_op jit(solution)/shard_map/dot_general | solution.py:120
  377.2 6.2 %copy.166 = bf16[1024,16,1,64]{3,1,2,0:T(8,128)(2,1)} copy(bf16[1024,16,1,64]{0,3,1,2:T(8,128)(2,1)} %bitcast.134) | data formatting | bytes 4194304 | tf_op jit(solution)/shard_map/reshape | solution.py:123
  383.3 7.6 %reshape.223 = bf16[8,2,65536]{2,1,0:T(2,128)(2,1)} reshape(bf16[1024,1,16,64]{3,2,1,0:T(8,128)(2,1)} %bitcast.119) | data formatting | bytes 4194304
  390.9 4.6 all-to-all-start.3
  395.5 1.0 copy.169
  396.5 2.3 copy.173
  398.8 5.7 %multiply_convert_fusion.1 = bf16[4,128,8,128]{3,1,2,0:T(8,128)(2,1)} fusion(bf16[1024,4,128,1]{0,2,3,1:T(8,128)(2,1)S(1)} %bitcast.123, bf16[4,8,128,1024]{2,3,1,0:T(8,128)(2,1)} %fusion), kind=kOutput, calls=%fused_computation.35 | convolution fusion | flops 1074790400 | bytes 10485760 | tf_op jit(solution)/shard_map/gjqk,kgd->qgjd/dot_general | solution.py:102
  404.5 2.3 copy.174
  406.8 23.2 %all-to-all-done.3 = bf16[8,2,65536]{2,1,0:T(2,128)(2,1)} async-done(((bf16[8,2,65536]{2,1,0:T(2,128)(2,1)}), bf16[8,2,65536]{2,1,0:T(2,128)(2,1)}, u32[]{:S(2)}, u32[]{:S(2)}) %all-to-all-start.3) | async-done | bytes 2097184 | tf_op jit(solution)/shard_map/all_to_all | solution.py:124
  430.0 7.4 %reshape.224 = bf16[1024,1,16,64]{3,2,1,0:T(8,128)(2,1)} reshape(bf16[8,2,65536]{2,1,0:T(2,128)(2,1)} %all-to-all-done.3) | data formatting | bytes 4194304
  437.4 5.4 copy.167
  442.8 2.1 convert_element_type.146
  444.9 1.0 copy.195
  445.9 0.7 copy.168
  446.7 1.4 copy-done
  448.1 0.1 copy-done.4
  448.2 4.8 multiply_reduce_fusion
  453.1 4.4 fusion.16
  457.4 4.1 copy.175
  461.5 0.2 copy.172
  461.7 0.1 reduce_sum.72
  461.8 53.5 %psum.14 = f32[8192]{0:T(1024)S(1)} all-reduce(f32[8192]{0:T(1024)S(1)} %reduce_sum.72), channel_id=1, replica_groups=mesh['blk'=16,'seq'=8] {'blk'}, use_global_device_ids=true, to_apply=%region_9.10 | all-reduce | flops 8192 | bytes 65536 | tf_op jit(solution)/shard_map/psum | solution.py:128
  515.3 42.2 %psum.15 = f32[8192]{0:T(1024)} all-reduce(f32[8192]{0:T(1024)S(1)} %psum.14), channel_id=1, replica_groups=mesh['blk'=16,'seq'=8] {'seq'}, use_global_device_ids=true, to_apply=%region_10.11 | all-reduce | flops 8192 | bytes 65536 | tf_op jit(solution)/shard_map/psum | solution.py:128
  (26 shorter events, 0.2 us)
Async XLA Ops:
  7.2 56.0 %all-gather.5.cloned.1.call-start = ((), (), s32[]{:S(2)}) async-start(), calls=%async_computation.5 | async-start | bytes 2228224 | tf_op jit(solution)/shard_map/all_gather | solution.py:45
  7.9 5.5 copy-start.7
  7.9 171.5 %all-gather.7.cloned.1.call-start = ((), (), s32[]{:S(2)}) async-start(), calls=%async_computation.6 | async-start | bytes 2359296 | tf_op jit(solution)/shard_map/all_gather | solution.py:69
  124.8 3.5 copy-start.5
  124.8 7.0 %copy-start.8 = (s32[1,128]{1,0:T(1,128)S(1)}, s32[1,128]{1,0:T(1,128)}, u32[]{:S(2)}) copy-start(s32[1,128]{1,0:T(1,128)} %param.9) | copy-start | bytes 1540
  128.2 236.5 %all-gather.9.cloned.1.call-start = ((), (), s32[]{:S(2)}) async-start(), calls=%async_computation.7 | async-start | bytes 2359296 | tf_op jit(solution)/shard_map/all_gather | solution.py:111
  195.2 8.7 %copy-start.6 = (bf16[1024,512]{0,1:T(8,128)(2,1)S(1)}, bf16[1024,512]{0,1:T(8,128)(2,1)}, u32[]{:S(2)}) copy-start(bf16[1024,512]{0,1:T(8,128)(2,1)} %copy.154) | copy-start | bytes 3145732
  203.9 9.9 %copy-start.3 = (bf16[1,128,4096]{1,2,0:T(8,128)(2,1)S(1)}, bf16[1,128,4096]{1,2,0:T(8,128)(2,1)}, u32[]{:S(2)}) copy-start(bf16[1,128,4096]{1,2,0:T(8,128)(2,1)} %copy.156) | copy-start | bytes 3145732
  237.6 3.5 copy-start.1
  251.0 2.2 copy-start.2
  310.1 247.4 %reduce-scatter.2.cloned.1.call-start = ((), (), s32[]{:S(2)}) async-start(), calls=%async_computation.8 | async-start | bytes 4456448 | tf_op jit(solution)/shard_map/reduce_scatter | solution.py:114
  390.9 39.1 %all-to-all-start.3 = ((bf16[8,2,65536]{2,1,0:T(2,128)(2,1)}), bf16[8,2,65536]{2,1,0:T(2,128)(2,1)}, u32[]{:S(2)}, u32[]{:S(2)}) async-start(bf16[8,2,65536]{2,1,0:T(2,128)(2,1)} %reshape.223), calls=%async_computation.3 | async-start | bytes 4194304 | tf_op jit(solution)/shard_map/all_to_all | solution.py:124
  445.9 2.2 copy-start
  445.9 2.3 copy-start.4
Sparse Core Ops, SparseCore 0:
  9.7 53.4 all-gather.4
  128.4 50.9 all-gather.6
  310.2 54.5 all-gather.8
  371.4 73.1 reduce-scatter.1
